TPU v7x, 32 devices: a whole 2x2x4 slice. The times are simulated.
32 devices in a mesh: scen: 2 (over y), cell: 4 (over z), obs: 4 (over x, core).
Axes of the slice: x: 2, y: 2, z: 4, core: 2. Of those that a mesh axis runs over, the one named last changes fastest.
Arguments:
- prior: bfloat16 [400, 2048], P('scen', 'cell'), parts along dimension 0, may hold values from -6 to 6
- obs_block: int32 [4096], P('obs'), may hold values from 0 to 15
- obs_weight: bfloat16 [4096, 128], P('obs'), may hold values from -0.5 to 0.5
- observed: float32 [8192], P(('scen', 'obs')), parts along dimension 0, may hold values from -8 to 8
- obs_sigma: float32 [4096], P('obs'), may hold values from 0.5 to 1.5
- pert_seed: int32 [6, 200, 4096], P('scen', None, 'obs'), parts along dimension 0, may hold values from 0 to 1048575
Outputs:
- posterior: bfloat16 [400, 2048], P('scen', 'cell'), parts along dimension 0
- post_predicted: float32 [400, 4096], P('scen', 'obs'), parts along dimension 0
There are 2 independent parts, one for each index of `scen`. A program takes and returns all parts, laid end to end along the dimension named above; an argument that names none is the same for every part. Nothing has to cross between parts.
All inputs are finite; a program needn't handle non-finite values.
Results may differ from a plain program's by a relative error of at most 0.0013.
Values sent between devices are 32-bit elements; how exact they have to be, the bound alone decides.
A program may use at most 64 MiB of HBM per device.

v0:
```python
import jax
import jax.numpy as jnp
from jax import lax
from jax.sharding import PartitionSpec as P

BLK = 128
ITERS = 3


def local_partial(param_field, local_index, weights):
    members = param_field.shape[0]
    nblocks = param_field.shape[1] // BLK
    blocks = param_field.reshape(members, nblocks, BLK)
    obs_count = local_index.shape[0]
    groups = obs_count // 64
    indices = local_index.reshape(groups, 64)
    group_weights = weights.reshape(groups, 64, BLK)

    def one_group(operands):
        group_index, group_weight = operands
        picked = jnp.take(blocks, group_index, axis=1)
        return jnp.sum(picked * group_weight[None], axis=2)

    result = lax.map(one_group, (indices, group_weights))
    return jnp.transpose(result, (1, 0, 2)).reshape(members, obs_count)


def per_device(prior, obs_block, obs_weight, observed, obs_sigma, pert_seed):
    members = prior.shape[0]
    nblocks = prior.shape[1] // BLK
    hp = lax.Precision.HIGHEST
    first_block = lax.axis_index("cell") * nblocks
    local_block = obs_block - first_block
    inside = jnp.logical_and(local_block >= 0, local_block < nblocks)
    clipped = jnp.clip(local_block, 0, nblocks - 1)
    weights = obs_weight.astype(jnp.float32) * inside[:, None].astype(jnp.float32)
    param_field = prior.astype(jnp.float32)
    inflation = jnp.float32(ITERS)
    root_scale = jnp.sqrt(jnp.float32(members - 1.0))
    identity = jnp.eye(members, dtype=jnp.float32)
    partial_terms = local_partial(param_field, clipped, weights)
    predicted = lax.psum(partial_terms, "cell")
    for step_index in range(ITERS):
        noise = jnp.sqrt(jnp.float32(3.0)) * (
            (2.0 * pert_seed[step_index].astype(jnp.float32) + 1.0) / 1048576.0 - 1.0
        )
        misfit = observed[None, :] + jnp.sqrt(inflation) * obs_sigma[None, :] * noise - predicted
        dev_pred = predicted - jnp.mean(predicted, axis=0, keepdims=True)
        dev_field = param_field - jnp.mean(param_field, axis=0, keepdims=True)
        scaled_dev = dev_pred / (obs_sigma[None, :] * root_scale)
        scaled_misfit = misfit / obs_sigma[None, :]
        gram_matrix = jnp.dot(scaled_dev, scaled_dev.T, precision=hp)
        cross_term = jnp.dot(scaled_dev, scaled_misfit.T, precision=hp)
        gram_matrix, cross_term = lax.psum((gram_matrix, cross_term), "obs")
        factor = jnp.linalg.cholesky(gram_matrix + inflation * identity)
        member_weight = jax.scipy.linalg.cho_solve((factor, True), cross_term)
        param_field = param_field + jnp.dot(member_weight.T, dev_field, precision=hp) / root_scale
        predicted = predicted + jnp.dot(member_weight.T, dev_pred, precision=hp) / root_scale
    return (param_field.astype(jnp.bfloat16), predicted)


def solution(mesh):
    return jax.shard_map(
        per_device,
        mesh=mesh,
        in_specs=(
            P("scen", "cell"),
            P("obs"),
            P("obs", None),
            P(("scen", "obs")),
            P("obs"),
            P("scen", None, "obs"),
        ),
        out_specs=(P("scen", "cell"), P("scen", "obs")),
        check_vma=False,
    )
```

profile of v0, /device:TPU:0, one launch (start us, length us, event | category | flops | bytes accessed | tf_op | source)
XLA Modules:
  0.0 502.5 jit_solution(17134970231463933520)
XLA Ops:
  10.8 143.9 %while.14 = (s32[]{:T(128)}, f32[16,200,64]{1,2,0:T(8,128)S(1)}, s32[16,64]{1,0:T(8,128)S(1)}, f32[200,4,128]{2,0,1:T(8,128)S(1)}, f32[16,64,128]{2,1,0:T(8,128)S(1)}, /*index=5*/s32[]{:T(128)}) while((s32[]{:T(128)}, f32[16,200,64]{1,2,0:T(8,128)S(1)}, s32[16,64]{1,0:T(8,128)S(1)}, f32[200,4,128]{2,0,1:T(8,128)S(1)}, ...), condition=%wide.region_2.3_spmd, body=%wide.region_0.2_spmd.sunk | while | flops 4904002 | bytes 19946964 | solution.py:24
  10.9 3.7 gather_fusion
  14.6 5.2 %multiply_reduce_fusion.2 = f32[64,200]{1,0:T(8,128)S(1)} fusion(f32[64,200,128]{2,1,0:T(8,128)} %gather_fusion, f32[64,128]{1,0:T(8,128)S(1)} %dynamic-slice_bitcast_fusion.2, pred[64]{0:T(512)(128)(4,1)S(1)} %compare_and_fusion.2), kind=kLoop, calls=%fused_computation.1.clone.1 | loop fusion | flops 4902400 | bytes 6637632 | tf_op jit(solution)/shard_map/while/body/eval_jaxpr/reduce_sum | solution.py:22
  19.8 3.7 gather_fusion
  23.6 5.2 %multiply_reduce_fusion.2 = f32[64,200]{1,0:T(8,128)S(1)} fusion(f32[64,200,128]{2,1,0:T(8,128)} %gather_fusion, f32[64,128]{1,0:T(8,128)S(1)} %dynamic-slice_bitcast_fusion.2, pred[64]{0:T(512)(128)(4,1)S(1)} %compare_and_fusion.2), kind=kLoop, calls=%fused_computation.1.clone.1 | loop fusion | flops 4902400 | bytes 6637632 | tf_op jit(solution)/shard_map/while/body/eval_jaxpr/reduce_sum | solution.py:22
  28.8 3.7 gather_fusion
  32.6 5.2 %multiply_reduce_fusion.2 = f32[64,200]{1,0:T(8,128)S(1)} fusion(f32[64,200,128]{2,1,0:T(8,128)} %gather_fusion, f32[64,128]{1,0:T(8,128)S(1)} %dynamic-slice_bitcast_fusion.2, pred[64]{0:T(512)(128)(4,1)S(1)} %compare_and_fusion.2), kind=kLoop, calls=%fused_computation.1.clone.1 | loop fusion | flops 4902400 | bytes 6637632 | tf_op jit(solution)/shard_map/while/body/eval_jaxpr/reduce_sum | solution.py:22
  37.8 3.7 gather_fusion
  41.6 5.2 %multiply_reduce_fusion.2 = f32[64,200]{1,0:T(8,128)S(1)} fusion(f32[64,200,128]{2,1,0:T(8,128)} %gather_fusion, f32[64,128]{1,0:T(8,128)S(1)} %dynamic-slice_bitcast_fusion.2, pred[64]{0:T(512)(128)(4,1)S(1)} %compare_and_fusion.2), kind=kLoop, calls=%fused_computation.1.clone.1 | loop fusion | flops 4902400 | bytes 6637632 | tf_op jit(solution)/shard_map/while/body/eval_jaxpr/reduce_sum | solution.py:22
  46.8 3.7 gather_fusion
  50.6 5.2 %multiply_reduce_fusion.2 = f32[64,200]{1,0:T(8,128)S(1)} fusion(f32[64,200,128]{2,1,0:T(8,128)} %gather_fusion, f32[64,128]{1,0:T(8,128)S(1)} %dynamic-slice_bitcast_fusion.2, pred[64]{0:T(512)(128)(4,1)S(1)} %compare_and_fusion.2), kind=kLoop, calls=%fused_computation.1.clone.1 | loop fusion | flops 4902400 | bytes 6637632 | tf_op jit(solution)/shard_map/while/body/eval_jaxpr/reduce_sum | solution.py:22
  55.8 3.7 gather_fusion
  59.6 5.2 %multiply_reduce_fusion.2 = f32[64,200]{1,0:T(8,128)S(1)} fusion(f32[64,200,128]{2,1,0:T(8,128)} %gather_fusion, f32[64,128]{1,0:T(8,128)S(1)} %dynamic-slice_bitcast_fusion.2, pred[64]{0:T(512)(128)(4,1)S(1)} %compare_and_fusion.2), kind=kLoop, calls=%fused_computation.1.clone.1 | loop fusion | flops 4902400 | bytes 6637632 | tf_op jit(solution)/shard_map/while/body/eval_jaxpr/reduce_sum | solution.py:22
  64.8 3.7 gather_fusion
  68.5 5.2 %multiply_reduce_fusion.2 = f32[64,200]{1,0:T(8,128)S(1)} fusion(f32[64,200,128]{2,1,0:T(8,128)} %gather_fusion, f32[64,128]{1,0:T(8,128)S(1)} %dynamic-slice_bitcast_fusion.2, pred[64]{0:T(512)(128)(4,1)S(1)} %compare_and_fusion.2), kind=kLoop, calls=%fused_computation.1.clone.1 | loop fusion | flops 4902400 | bytes 6637632 | tf_op jit(solution)/shard_map/while/body/eval_jaxpr/reduce_sum | solution.py:22
  73.8 3.7 gather_fusion
  77.5 5.2 %multiply_reduce_fusion.2 = f32[64,200]{1,0:T(8,128)S(1)} fusion(f32[64,200,128]{2,1,0:T(8,128)} %gather_fusion, f32[64,128]{1,0:T(8,128)S(1)} %dynamic-slice_bitcast_fusion.2, pred[64]{0:T(512)(128)(4,1)S(1)} %compare_and_fusion.2), kind=kLoop, calls=%fused_computation.1.clone.1 | loop fusion | flops 4902400 | bytes 6637632 | tf_op jit(solution)/shard_map/while/body/eval_jaxpr/reduce_sum | solution.py:22
  82.8 3.7 gather_fusion
  86.5 5.2 %multiply_reduce_fusion.2 = f32[64,200]{1,0:T(8,128)S(1)} fusion(f32[64,200,128]{2,1,0:T(8,128)} %gather_fusion, f32[64,128]{1,0:T(8,128)S(1)} %dynamic-slice_bitcast_fusion.2, pred[64]{0:T(512)(128)(4,1)S(1)} %compare_and_fusion.2), kind=kLoop, calls=%fused_computation.1.clone.1 | loop fusion | flops 4902400 | bytes 6637632 | tf_op jit(solution)/shard_map/while/body/eval_jaxpr/reduce_sum | solution.py:22
  91.8 3.7 gather_fusion
  95.5 5.2 %multiply_reduce_fusion.2 = f32[64,200]{1,0:T(8,128)S(1)} fusion(f32[64,200,128]{2,1,0:T(8,128)} %gather_fusion, f32[64,128]{1,0:T(8,128)S(1)} %dynamic-slice_bitcast_fusion.2, pred[64]{0:T(512)(128)(4,1)S(1)} %compare_and_fusion.2), kind=kLoop, calls=%fused_computation.1.clone.1 | loop fusion | flops 4902400 | bytes 6637632 | tf_op jit(solution)/shard_map/while/body/eval_jaxpr/reduce_sum | solution.py:22
  100.8 3.7 gather_fusion
  104.5 5.2 %multiply_reduce_fusion.2 = f32[64,200]{1,0:T(8,128)S(1)} fusion(f32[64,200,128]{2,1,0:T(8,128)} %gather_fusion, f32[64,128]{1,0:T(8,128)S(1)} %dynamic-slice_bitcast_fusion.2, pred[64]{0:T(512)(128)(4,1)S(1)} %compare_and_fusion.2), kind=kLoop, calls=%fused_computation.1.clone.1 | loop fusion | flops 4902400 | bytes 6637632 | tf_op jit(solution)/shard_map/while/body/eval_jaxpr/reduce_sum | solution.py:22
  109.8 3.7 gather_fusion
  113.5 5.2 %multiply_reduce_fusion.2 = f32[64,200]{1,0:T(8,128)S(1)} fusion(f32[64,200,128]{2,1,0:T(8,128)} %gather_fusion, f32[64,128]{1,0:T(8,128)S(1)} %dynamic-slice_bitcast_fusion.2, pred[64]{0:T(512)(128)(4,1)S(1)} %compare_and_fusion.2), kind=kLoop, calls=%fused_computation.1.clone.1 | loop fusion | flops 4902400 | bytes 6637632 | tf_op jit(solution)/shard_map/while/body/eval_jaxpr/reduce_sum | solution.py:22
  118.8 3.7 gather_fusion
  122.5 5.2 %multiply_reduce_fusion.2 = f32[64,200]{1,0:T(8,128)S(1)} fusion(f32[64,200,128]{2,1,0:T(8,128)} %gather_fusion, f32[64,128]{1,0:T(8,128)S(1)} %dynamic-slice_bitcast_fusion.2, pred[64]{0:T(512)(128)(4,1)S(1)} %compare_and_fusion.2), kind=kLoop, calls=%fused_computation.1.clone.1 | loop fusion | flops 4902400 | bytes 6637632 | tf_op jit(solution)/shard_map/while/body/eval_jaxpr/reduce_sum | solution.py:22
  131.5 5.2 %multiply_reduce_fusion.2 = f32[64,200]{1,0:T(8,128)S(1)} fusion(f32[64,200,128]{2,1,0:T(8,128)} %gather_fusion, f32[64,128]{1,0:T(8,128)S(1)} %dynamic-slice_bitcast_fusion.2, pred[64]{0:T(512)(128)(4,1)S(1)} %compare_and_fusion.2), kind=kLoop, calls=%fused_computation.1.clone.1 | loop fusion | flops 4902400 | bytes 6637632 | tf_op jit(solution)/shard_map/while/body/eval_jaxpr/reduce_sum | solution.py:22
  136.7 3.7 gather_fusion
  140.5 5.2 %multiply_reduce_fusion.2 = f32[64,200]{1,0:T(8,128)S(1)} fusion(f32[64,200,128]{2,1,0:T(8,128)} %gather_fusion, f32[64,128]{1,0:T(8,128)S(1)} %dynamic-slice_bitcast_fusion.2, pred[64]{0:T(512)(128)(4,1)S(1)} %compare_and_fusion.2), kind=kLoop, calls=%fused_computation.1.clone.1 | loop fusion | flops 4902400 | bytes 6637632 | tf_op jit(solution)/shard_map/while/body/eval_jaxpr/reduce_sum | solution.py:22
  145.7 3.7 gather_fusion
  149.5 5.2 %multiply_reduce_fusion.2 = f32[64,200]{1,0:T(8,128)S(1)} fusion(f32[64,200,128]{2,1,0:T(8,128)} %gather_fusion, f32[64,128]{1,0:T(8,128)S(1)} %dynamic-slice_bitcast_fusion.2, pred[64]{0:T(512)(128)(4,1)S(1)} %compare_and_fusion.2), kind=kLoop, calls=%fused_computation.1.clone.1 | loop fusion | flops 4902400 | bytes 6637632 | tf_op jit(solution)/shard_map/while/body/eval_jaxpr/reduce_sum | solution.py:22
  156.1 47.5 %all-reduce.11.cloned.1.call-done = f32[200,1024]{1,0:T(8,128)} async-done(((f32[200,1024]{1,0:T(8,128)}), f32[200,1024]{1,0:T(8,128)}) %all-reduce.11.cloned.1.call-update) | async-done | bytes 819216 | tf_op jit(solution)/shard_map/psum | solution.py:42
  211.9 31.3 %all-reduce.17.cloned.1.call-done = (f32[200,200]{1,0:T(8,128)}, f32[200,200]{0,1:T(8,128)}) async-done(((f32[200,200]{1,0:T(8,128)}, f32[200,200]{0,1:T(8,128)}), (f32[200,200]{1,0:T(8,128)}, f32[200,200]{0,1:T(8,128)})) %all-reduce.17.cloned.1.call-update) | async-done | bytes 320016 | tf_op jit(solution)/shard_map/psum | solution.py:54
  245.2 11.7 %cholesky.182 = f32[128,128]{1,0:T(8,128)S(1)} custom-call(f32[128,128]{1,0:T(8,128)S(1)} %cholesky.292), custom_call_target="Cholesky" | custom-call | tf_op jit(solution)/shard_map/jit(cholesky)/cholesky | solution.py:55
  257.0 9.8 %custom-call.17 = f32[1,128,128]{1,2,0:T(8,128)S(1)} custom-call(f32[1,128,128]{2,1,0:T(8,128)S(1)} %get-tuple-element.95), custom_call_target="InvertDiagBlocksLowerTriangular" | custom-call | tf_op jit(solution)/shard_map/jit(cholesky)/cholesky | solution.py:55
  267.2 6.6 %cholesky.202 = f32[72,72]{1,0:T(8,128)S(1)} custom-call(f32[72,72]{1,0:T(8,128)S(1)} %convolution_subtract_fusion.8), custom_call_target="Cholesky" | custom-call | tf_op jit(solution)/shard_map/jit(cholesky)/cholesky | solution.py:55
  276.6 19.8 %custom-call.18 = f32[2,128,128]{1,2,0:T(8,128)S(1)} custom-call(f32[2,128,128]{2,1,0:T(8,128)S(1)} %pad_maximum_fusion.9), custom_call_target="InvertDiagBlocksLowerTriangular" | custom-call | tf_op jit(solution)/shard_map/jit(_cho_solve)/triangular_solve | solution.py:56
  306.6 32.8 %all-reduce.15.cloned.1.call-done = (f32[200,200]{1,0:T(8,128)}, f32[200,200]{0,1:T(8,128)}) async-done(((f32[200,200]{1,0:T(8,128)}, f32[200,200]{0,1:T(8,128)}), (f32[200,200]{1,0:T(8,128)}, f32[200,200]{0,1:T(8,128)})) %all-reduce.15.cloned.1.call-update) | async-done | bytes 320016 | tf_op jit(solution)/shard_map/psum | solution.py:54
  341.5 11.7 %cholesky.220 = f32[128,128]{1,0:T(8,128)S(1)} custom-call(f32[128,128]{1,0:T(8,128)S(1)} %cholesky.295), custom_call_target="Cholesky" | custom-call | tf_op jit(solution)/shard_map/jit(cholesky)/cholesky | solution.py:55
  353.3 9.8 %custom-call.19 = f32[1,128,128]{1,2,0:T(8,128)S(1)} custom-call(f32[1,128,128]{2,1,0:T(8,128)S(1)} %get-tuple-element.93), custom_call_target="InvertDiagBlocksLowerTriangular" | custom-call | tf_op jit(solution)/shard_map/jit(cholesky)/cholesky | solution.py:55
  363.5 6.6 %cholesky.240 = f32[72,72]{1,0:T(8,128)S(1)} custom-call(f32[72,72]{1,0:T(8,128)S(1)} %convolution_subtract_fusion.7), custom_call_target="Cholesky" | custom-call | tf_op jit(solution)/shard_map/jit(cholesky)/cholesky | solution.py:55
  372.9 19.9 %custom-call.20 = f32[2,128,128]{1,2,0:T(8,128)S(1)} custom-call(f32[2,128,128]{2,1,0:T(8,128)S(1)} %pad_maximum_fusion.10), custom_call_target="InvertDiagBlocksLowerTriangular" | custom-call | tf_op jit(solution)/shard_map/jit(_cho_solve)/triangular_solve | solution.py:56
  402.7 32.5 %all-reduce.13.cloned.1.call-done = (f32[200,200]{1,0:T(8,128)}, f32[200,200]{0,1:T(8,128)}) async-done(((f32[200,200]{1,0:T(8,128)}, f32[200,200]{0,1:T(8,128)}), (f32[200,200]{1,0:T(8,128)}, f32[200,200]{0,1:T(8,128)})) %all-reduce.13.cloned.1.call-update) | async-done | bytes 320016 | tf_op jit(solution)/shard_map/psum | solution.py:54
  437.3 11.7 %cholesky.258 = f32[128,128]{1,0:T(8,128)S(1)} custom-call(f32[128,128]{1,0:T(8,128)S(1)} %cholesky.298), custom_call_target="Cholesky" | custom-call | tf_op jit(solution)/shard_map/jit(cholesky)/cholesky | solution.py:55
  449.1 9.8 %custom-call.21 = f32[1,128,128]{1,2,0:T(8,128)S(1)} custom-call(f32[1,128,128]{2,1,0:T(8,128)S(1)} %get-tuple-element.91), custom_call_target="InvertDiagBlocksLowerTriangular" | custom-call | tf_op jit(solution)/shard_map/jit(cholesky)/cholesky | solution.py:55
  459.3 6.8 %cholesky.278 = f32[72,72]{1,0:T(8,128)S(1)} custom-call(f32[72,72]{1,0:T(8,128)S(1)} %convolution_subtract_fusion.6), custom_call_target="Cholesky" | custom-call | tf_op jit(solution)/shard_map/jit(cholesky)/cholesky | solution.py:55
  468.9 19.7 %custom-call.22 = f32[2,128,128]{1,2,0:T(8,128)S(1)} custom-call(f32[2,128,128]{2,1,0:T(8,128)S(1)} %pad_maximum_fusion.11), custom_call_target="InvertDiagBlocksLowerTriangular" | custom-call | tf_op jit(solution)/shard_map/jit(_cho_solve)/triangular_solve | solution.py:56
  (195 shorter events, 56.3 us)
Async XLA Ops:
  7.2 196.4 %all-reduce.11.cloned.1.call-start = ((), (), s32[]{:S(2)}) async-start(), calls=%async_computation | async-start | bytes 1638400 | tf_op jit(solution)/shard_map/psum | solution.py:42
  10.8 145.2 %copy-start.1 = (bf16[200,512]{1,0:T(8,128)(2,1)S(1)}, bf16[200,512]{1,0:T(8,128)(2,1)}, u32[]{:S(2)}) copy-start(bf16[200,512]{1,0:T(8,128)(2,1)} %param.11) | copy-start | bytes 614404
  10.8 145.3 %copy-start.2 = (f32[1024]{0:T(1024)S(1)}, f32[1024]{0:T(1024)}, u32[]{:S(2)}) copy-start(f32[1024]{0:T(1024)} %param.15) | copy-start | bytes 12292
  154.7 53.1 %copy-start.3 = (f32[1024]{0:T(1024)S(1)}, f32[1024]{0:T(1024)}, u32[]{:S(2)}) copy-start(f32[1024]{0:T(1024)} %param.14) | copy-start | bytes 12292
  155.9 87.2 %all-reduce.17.cloned.1.call-start = ((), (), s32[]{:S(2)}) async-start(), calls=%async_computation.3 | async-start | bytes 819200 | tf_op jit(solution)/shard_map/psum | solution.py:54
  207.8 92.5 %copy-start = (f32[200,1024]{1,0:T(8,128)S(1)}, f32[200,1024]{1,0:T(8,128)}, u32[]{:S(2)}) copy-start(f32[200,1024]{1,0:T(8,128)} %all-reduce.11.cloned.1.call-done) | copy-start | bytes 2457604
  211.3 128.2 %all-reduce.15.cloned.1.call-start = ((), (), s32[]{:S(2)}) async-start(), calls=%async_computation.2 | async-start | bytes 819200 | tf_op jit(solution)/shard_map/psum | solution.py:54
  306.4 128.9 %all-reduce.13.cloned.1.call-start = ((), (), s32[]{:S(2)}) async-start(), calls=%async_computation.1 | async-start | bytes 819200 | tf_op jit(solution)/shard_map/psum | solution.py:54
Sparse Core Ops, SparseCore 0:
  156.1 47.4 all-reduce.10
  211.4 31.6 all-reduce.16
  306.5 32.9 all-reduce.14
  402.3 32.9 all-reduce.12
where the time goes:
time: 508 us; the launch traced here: 503 us
  other arithmetic  242 us (48%)
  waiting for transfers between devices  144 us (28%)
  local copies, waits for them, and re-layouts  61.6 us (12%)
  matrix products  33.9 us (7%)
  between operations  18.7 us (4%)
    psum x3, waiting for transfers between devices, per_device(): gram_matrix, cross_term = lax.psum((gram_matrix, cross_term), 'obs')  96.6 us
    another operation x21, other arithmetic, per_device(): factor = jnp.linalg.cholesky(gram_matrix + inflation * identity)  88.6 us
    reduce_sum x16, other arithmetic, one_group(): return jnp.sum(picked * group_weight[None], axis=2)  83 us
    another operation x14, other arithmetic, per_device(): member_weight = jax.scipy.linalg.cho_solve((factor, True), cross_term)  59.8 us
    gather x16, local copies, waits for them, and re-layouts, one_group(): picked = jnp.take(blocks, group_index, axis=1)  59.3 us
    psum x1, waiting for transfers between devices, per_device(): predicted = lax.psum(partial_terms, 'cell')  47.5 us
    another operation x18, matrix products, per_device(): member_weight = jax.scipy.linalg.cho_solve((factor, True), cross_term)  11.1 us
  transfers between devices with their start and end apart: 4, of which 4 were waited for; matrix products, arithmetic and copies ran while one was open for 0% of the time, Pallas kernels for 0%

commit v1 on v0

v1 whole, which is shorter than its diff:
```python
import functools

import jax
import jax.numpy as jnp
from jax import lax
from jax.experimental import pallas as pl
from jax.experimental.pallas import tpu as pltpu
from jax.sharding import PartitionSpec as P

BLK = 128
ITERS = 3
MESH = pl.DeviceIdType.MESH
VM = pl.BlockSpec(memory_space=pltpu.VMEM)
NN = (((1,), (0,)), ((), ()))
NT = (((1,), (1,)), ((), ()))


def mm(a, b, dims):
    return lax.dot_general(a, b, dims, preferred_element_type=jnp.float32)


def split(x):
    hi = x.astype(jnp.bfloat16)
    return hi, (x - hi.astype(jnp.float32)).astype(jnp.bfloat16)


def dot3(a, b, dims):
    ah, al = split(a)
    bh, bl = split(b)
    return mm(ah, bh, dims) + (mm(ah, bl, dims) + mm(al, bh, dims))


def dot_exact(a, b, dims):
    return lax.dot_general(a, b, dims, precision=lax.Precision.HIGHEST, preferred_element_type=jnp.float32)


def block_predictions(fields, weights, block):
    total = None
    for field, first in fields:
        for b in range(field.shape[1] // BLK):
            part = mm(field[:, b * BLK:(b + 1) * BLK].astype(jnp.bfloat16), weights[...], NT)
            here = block == first + b
            total = jnp.where(here, part, 0.0 if total is None else total)
    return total


def sums_kernel(n_cell, n_obs, prior, block, weights, observed, sigma, seeds, out, acc, fin, obs_recv, cell_recv,
                send_sem, recv_sem):
    members, width = prior.shape
    cell, obs = lax.axis_index("cell"), lax.axis_index("obs")
    bits = [1 << k for k in range(n_obs.bit_length() - 1)]
    barrier = pltpu.get_barrier_semaphore()
    for bit in bits:
        pl.semaphore_signal(barrier, inc=1, device_id={"obs": obs ^ bit}, device_id_type=MESH)
    for d in range(1, n_cell):
        pl.semaphore_signal(barrier, inc=1, device_id={"cell": lax.rem(cell + d, n_cell)}, device_id_type=MESH)

    nblocks = width // BLK
    first = cell * nblocks
    blk = block[...]
    predicted = block_predictions([(prior, first)], weights, blk)
    inside = jnp.logical_and(blk >= first, blk < first + nblocks)
    mean = jnp.mean(predicted, axis=0, keepdims=True)
    inv = 1.0 / sigma[...]
    dev = (predicted - mean) * jnp.where(inside, inv, 0.0)
    base = (observed[...] - mean) * inv + (3.0 / 1048576.0 - 3.0)
    ah, al = split(dev)
    scale = 1.0 / (members - 1.0)
    rows = acc.shape[1]

    def noisy(i):
        return split(base + seeds[i].astype(jnp.float32) * (6.0 / 1048576.0))

    def put(s, k, h, l):
        acc[s, k * members:(k + 1) * members, 0:members] = (
            mm(h, ah, NT) + (mm(h, al, NT) + mm(l, ah, NT))) * scale

    acc[...] = jnp.zeros_like(acc)

    nbit = len(bits)
    lens = [rows >> k for k in range(nbit + 1)]
    offs = [jnp.int32(0)]
    for k in range(nbit):
        offs.append(pl.multiple_of(offs[-1] + ((obs >> k) & 1) * lens[k + 1], 8))
    quarter, off = lens[-1], offs[-1]
    chunk = quarter // n_cell
    stages = 2 * nbit + 2
    obs_at = [0]
    for k in range(nbit):
        obs_at.append(obs_at[-1] + lens[k + 1])

    def copies(s, stage):
        made = []
        if stage < nbit:
            n = lens[stage + 1]
            src = pl.multiple_of(offs[stage] + (1 - ((obs >> stage) & 1)) * n, 8)
            made.append((acc.at[s, pl.ds(src, n)], obs_recv.at[s, pl.ds(obs_at[stage], n)], {"obs": obs ^ bits[stage]}))
        elif stage == nbit:
            for d in range(1, n_cell):
                to = lax.rem(cell + d, n_cell)
                src = pl.multiple_of(off + to * chunk, 8)
                made.append((acc.at[s, pl.ds(src, chunk)], cell_recv.at[s, d - 1], {"cell": to}))
        elif stage == nbit + 1:
            src = pl.multiple_of(off + cell * chunk, 8)
            for d in range(1, n_cell):
                to = lax.rem(cell + d, n_cell)
                made.append((fin.at[s, pl.ds(src, chunk)], fin.at[s, pl.ds(src, chunk)], {"cell": to}))
        else:
            k = stages - 1 - stage
            n = lens[k + 1]
            made.append((fin.at[s, pl.ds(offs[k + 1], n)], fin.at[s, pl.ds(offs[k + 1], n)], {"obs": obs ^ bits[k]}))
        return [
            pltpu.make_async_remote_copy(src_ref=a, dst_ref=b, send_sem=send_sem.at[s, stage, j],
                                         recv_sem=recv_sem.at[s, stage, j], device_id=to, device_id_type=MESH)
            for j, (a, b, to) in enumerate(made)
        ]

    flights = {}

    def start(s, stage):
        flights[s, stage] = copies(s, stage)
        for c in flights[s, stage]:
            c.start()

    def finish(s, stage):
        for c in flights[s, stage]:
            c.wait()
        if stage < nbit:
            n = lens[stage + 1]
            mine = pl.ds(offs[stage + 1], n)
            acc[s, mine] = acc[s, mine] + obs_recv[s, pl.ds(obs_at[stage], n)]
        elif stage == nbit:
            mine = pl.ds(pl.multiple_of(off + cell * chunk, 8), chunk)
            total = acc[s, mine]
            for d in range(1, n_cell):
                total = total + cell_recv[s, d - 1]
            fin[s, mine] = total

    put(0, 0, ah, al)
    put(0, 1, *noisy(0))
    pl.semaphore_wait(barrier, len(bits) + n_cell - 1)
    start(0, 0)
    put(1, 0, *noisy(1))
    put(1, 1, *noisy(2))
    for stage in range(stages + 1):
        if stage < stages:
            finish(0, stage)
            if stage + 1 < stages:
                start(0, stage + 1)
        if stage > 0:
            finish(1, stage - 1)
        if stage < stages:
            start(1, stage)
    for s in range(2):
        for k in range(2):
            out[2 * s + k] = fin[s, k * members:(k + 1) * members, 0:members]


def solve_kernel(sums, result, stack, dev_op):
    members = result.shape[0]
    row = lax.broadcasted_iota(jnp.int32, (members, members), 0)
    col = lax.broadcasted_iota(jnp.int32, (members, members), 1)
    eye = jnp.where(row == col, 1.0, 0.0)
    inflation = float(ITERS)
    up, down = pl.ds(0, members), pl.ds(members, members)

    def solve(gram, cross):
        system = gram + inflation * eye
        bound = jnp.max(jnp.sum(jnp.abs(system), axis=1))
        scale = 2.0 / (inflation + bound)
        stack[up] = eye - scale * system
        stack[down] = scale * cross

        def loop(dot):
            def body(carry):
                step, _ = carry
                residue = stack[up]
                size = jnp.sum(residue * residue)
                moved = dot(stack[...], residue, NN)
                stack[down] = stack[down] + moved[members:]
                stack[up] = moved[:members]
                return step + 1, size

            lax.while_loop(lambda c: jnp.logical_and(c[0] < 64, c[1] > 1e-6), body, (jnp.int32(0), jnp.float32(1e9)))

        pl.when(bound <= 300.0)(lambda: loop(dot3))
        pl.when(jnp.logical_not(bound <= 300.0))(lambda: loop(dot_exact))
        return stack[down]

    gram0 = sums[0]
    change = solve(gram0, sums[1] - gram0)
    change = change - jnp.mean(change, axis=1, keepdims=True)
    result[...] = change
    for i in range(1, ITERS):
        change = result[...]
        dev_op[...] = eye + change - jnp.mean(eye + change, axis=0, keepdims=True)
        stack[up] = sums[0] + dot3(change, sums[0], NN)
        stack[down] = sums[1 + i]
        both = dot3(stack[...], dev_op[...], NT)
        v = both[:members]
        z = solve(v - jnp.mean(v, axis=0, keepdims=True), both[members:] - v)
        result[...] = result[...] + dot3(z, dev_op[...], NN)


def final_kernel(n_cell, change, prior, block, weights, *refs):
    others, (posterior, post_predicted) = refs[:n_cell - 1], refs[n_cell - 1:]
    cell = lax.axis_index("cell")
    nblocks = prior.shape[1] // BLK
    fields = [(prior, cell * nblocks)]
    fields += [(other, lax.rem(cell + d + 1, n_cell) * nblocks) for d, other in enumerate(others)]
    predicted = block_predictions(fields, weights, block[...])
    field = prior[...].astype(jnp.float32)
    shift = change[...]
    field_dev = field - jnp.mean(field, axis=0, keepdims=True)
    posterior[...] = (field + dot3(shift, field_dev, NN)).astype(jnp.bfloat16)
    pred_dev = predicted - jnp.mean(predicted, axis=0, keepdims=True)
    post_predicted[...] = predicted + dot3(shift, pred_dev, NN)


def per_device(n_cell, n_obs, prior, obs_block, obs_weight, observed, obs_sigma, pert_seed):
    members, width = prior.shape
    count = obs_block.shape[0]
    block, observed, sigma = (x.reshape(1, count) for x in (obs_block, observed, obs_sigma))
    wide = prior.astype(jnp.float32)
    others = []
    for d in range(1, n_cell):
        others.append(lax.ppermute(wide, "cell", [((i + d) % n_cell, i) for i in range(n_cell)]))
    unit = 8 * n_cell * n_obs
    rows = -(-2 * members // unit) * unit
    lanes = -(-members // 128) * 128
    quarter = rows // n_obs
    stages = 2 * (n_obs.bit_length() - 1) + 2
    f32 = jnp.float32
    sums = pl.pallas_call(
        functools.partial(sums_kernel, n_cell, n_obs),
        out_shape=jax.ShapeDtypeStruct((4, members, members), f32),
        in_specs=[VM] * 6,
        out_specs=VM,
        scratch_shapes=[
            pltpu.VMEM((2, rows, lanes), f32),
            pltpu.VMEM((2, rows, lanes), f32),
            pltpu.VMEM((2, rows, lanes), f32),
            pltpu.VMEM((2, n_cell - 1, quarter // n_cell, lanes), f32),
            pltpu.SemaphoreType.DMA((2, stages, n_cell - 1)),
            pltpu.SemaphoreType.DMA((2, stages, n_cell - 1)),
        ],
        compiler_params=pltpu.CompilerParams(collective_id=0, has_side_effects=True, vmem_limit_bytes=48 << 20),
        cost_estimate=pl.CostEstimate(flops=2_000_000_000, bytes_accessed=4_000_000, transcendentals=0),
        name="sums",
    )(prior, block, obs_weight, observed, sigma, pert_seed)
    change = pl.pallas_call(
        solve_kernel,
        out_shape=jax.ShapeDtypeStruct((members, members), f32),
        in_specs=[VM],
        out_specs=VM,
        scratch_shapes=[pltpu.VMEM((2 * members, members), f32), pltpu.VMEM((members, members), f32)],
        cost_estimate=pl.CostEstimate(flops=20_000_000_000, bytes_accessed=60_000_000, transcendentals=0),
        name="solve",
    )(sums)
    return pl.pallas_call(
        functools.partial(final_kernel, n_cell),
        out_shape=(jax.ShapeDtypeStruct((members, width), jnp.bfloat16),
                   jax.ShapeDtypeStruct((members, count), f32)),
        in_specs=[VM] * (4 + len(others)),
        out_specs=(VM, VM),
        name="final",
    )(change, prior, block, obs_weight, *others)


def solution(mesh):
    return jax.shard_map(
        functools.partial(per_device, mesh.shape["cell"], mesh.shape["obs"]),
        mesh=mesh,
        in_specs=(
            P("scen", "cell"),
            P("obs"),
            P("obs", None),
            P(("scen", "obs")),
            P("obs"),
            P("scen", None, "obs"),
        ),
        out_specs=(P("scen", "cell"), P("scen", "obs")),
        check_vma=False,
    )
```

time: 508 us -> 86.5 us (0.17); the launches traced: 503 us -> 86.4 us
  other arithmetic: 242 us -> 0.97 us
  waiting for transfers between devices: 144 us -> 0.01 us
  Pallas kernels: 0 us -> 69.5 us
  local copies, waits for them, and re-layouts: 61.6 us -> 8.16 us
  matrix products: 33.9 us -> 0 us
  between operations: 18.7 us -> 0.68 us
  starting transfers between devices: 0.9 us -> 7.04 us
    another operation x35 -> x0, other arithmetic: 148 us -> none  [the longest x21 88.6 us: per_device(): factor = jnp.linalg.cholesky(gram_matrix + inflation * identity)]
    psum x4 -> x0, waiting for transfers between devices: 144 us -> none  [the longest x3 96.6 us: per_device(): gram_matrix, cross_term = lax.psum((gram_matrix, cross_term), 'obs')]
    reduce_sum x18 -> x0, other arithmetic: 84.3 us -> none  [the longest x16 83 us: one_group(): return jnp.sum(picked * group_weight[None], axis=2)]
    pallas_call x0 -> x3, Pallas kernels: none -> 69.5 us  [the longest x1 49.7 us: per_device(): pl.pallas_call(functools.partial(sums_kernel, n_cell, n_obs), out_shape=j...]
    gather x16 -> x0, local copies, waits for them, and re-layouts: 59.3 us -> none  [one_group(): picked = jnp.take(blocks, group_index, axis=1)]
    dot_general x12 -> x0, matrix products: 21.6 us -> none  [the longest x3 9.33 us: per_device(): cross_term = jnp.dot(scaled_dev, scaled_misfit.T, precision=hp)]
    another operation x24 -> x0, matrix products: 12.4 us -> none  [the longest x18 11.1 us: per_device(): member_weight = jax.scipy.linalg.cho_solve((factor, True), cross_term)]
    unnamed x8 -> x20, local copies, waits for them, and re-layouts: 0.02 us -> 8.16 us
  transfers between devices with their start and end apart: 4 -> 3, of which waited for: 4 -> 0; matrix products, arithmetic and copies ran while one was open for 0% -> 0% of each run, Pallas kernels for 0% -> 75%
where the time goes in v1:
time: 86.5 us; the launch traced here: 86.4 us
  Pallas kernels  69.5 us (80%)
  local copies, waits for them, and re-layouts  8.16 us (9%)
  starting transfers between devices  7.04 us (8%)
  other arithmetic  0.97 us (1%)
    pallas_call x1, Pallas kernels, per_device(): pl.pallas_call(functools.partial(sums_kernel, n_cell, n_obs), out_shape=j...  49.7 us
    pallas_call x1, Pallas kernels, per_device(): pl.pallas_call(solve_kernel, out_shape=jax.ShapeDtypeStruct((members, mem...  14.8 us
    unnamed x20, local copies, waits for them, and re-layouts  8.16 us
    ppermute x3, starting transfers between devices, per_device(): lax.ppermute(wide, 'cell', [((i + d) % n_cell, i) for i in range(n_cell)])  7.04 us
    pallas_call x1, Pallas kernels, per_device(): pl.pallas_call(functools.partial(final_kernel, n_cell), out_shape=(jax.Sh...  5.01 us
  transfers between devices with their start and end apart: 3, of which 0 were waited for; matrix products, arithmetic and copies ran while one was open for 0% of the time, Pallas kernels for 75%

profile of v1, /device:TPU:0, one launch (start us, length us, event | category | flops | bytes accessed | tf_op | source)
XLA Modules:
  0.0 86.4 jit_solution(11720459935534361346)
XLA Ops:
  0.6 1.0 %convert_element_type.3 = f32[200,512]{1,0:T(8,128)S(1)} convert(bf16[200,512]{1,0:T(8,128)(2,1)} %prior.3) | non-fusion elementwise | flops 102400 | bytes 614400 | tf_op jit(solution)/shard_map/convert_element_type | solution.py:224
  1.6 3.1 %collective-permute-start.2 = (f32[200,512]{1,0:T(8,128)S(1)}, f32[200,512]{1,0:T(8,128)S(1)}, u32[]{:S(2)}, u32[]{:S(2)}) collective-permute-start(f32[200,512]{1,0:T(8,128)S(1)} %convert_element_type.3), channel_id=1, source_target_pairs={{12,0},{0,4},{4,8},{8,12},{13,1},{1,5},{5,9},{9,13},{14,2},{2,6},{... | collective-permute-start | bytes 1228808 | tf_op jit(solution)/shard_map/ppermute | solution.py:227
  4.7 2.6 %collective-permute-start.1 = (f32[200,512]{1,0:T(8,128)S(1)}, f32[200,512]{1,0:T(8,128)S(1)}, u32[]{:S(2)}, u32[]{:S(2)}) collective-permute-start(f32[200,512]{1,0:T(8,128)S(1)} %convert_element_type.3), channel_id=1, source_target_pairs={{8,0},{12,4},{0,8},{4,12},{9,1},{13,5},{1,9},{5,13},{10,2},{14,6},... | collective-permute-start | bytes 1228808 | tf_op jit(solution)/shard_map/ppermute | solution.py:227
  7.3 1.3 %collective-permute-start = (f32[200,512]{1,0:T(8,128)S(1)}, f32[200,512]{1,0:T(8,128)S(1)}, u32[]{:S(2)}, u32[]{:S(2)}) collective-permute-start(f32[200,512]{1,0:T(8,128)S(1)} %convert_element_type.3), channel_id=1, source_target_pairs={{4,0},{8,4},{12,8},{0,12},{5,1},{9,5},{13,9},{1,13},{6,2},{10,6},{... | collective-permute-start | bytes 1228808 | tf_op jit(solution)/shard_map/ppermute | solution.py:227
  8.6 0.0 copy-start
  8.6 0.9 %copy-done = bf16[200,512]{1,0:T(8,128)(2,1)S(1)} copy-done((bf16[200,512]{1,0:T(8,128)(2,1)S(1)}, bf16[200,512]{1,0:T(8,128)(2,1)}, u32[]{:S(2)}) %copy-start) | copy-done | bytes 204824
  9.6 0.0 copy-start.1
  9.6 0.9 %copy-done.1 = bf16[1024,128]{1,0:T(8,128)(2,1)S(1)} copy-done((bf16[1024,128]{1,0:T(8,128)(2,1)S(1)}, bf16[1024,128]{1,0:T(8,128)(2,1)}, u32[]{:S(2)}) %copy-start.1) | copy-done | bytes 262168
  10.5 0.0 copy-start.2
  10.5 0.7 copy-done.2
  11.2 0.0 copy-start.3
  11.2 1.7 %copy-done.3 = s32[3,200,1024]{2,1,0:T(8,128)S(1)} copy-done((s32[3,200,1024]{2,1,0:T(8,128)S(1)}, s32[3,200,1024]{2,1,0:T(8,128)}, u32[]{:S(2)}) %copy-start.3) | copy-done | bytes 2457624
  12.9 0.0 copy-start.4
  12.9 0.7 copy-done.4
  13.6 0.0 copy-start.5
  13.6 0.7 copy-done.5
  14.3 49.7 %sums.1 = f32[4,200,200]{2,1,0:T(8,128)S(1)} custom-call(bf16[200,512]{1,0:T(8,128)(2,1)S(1)} %copy-done, s32[1,1024]{1,0:T(1,128)S(1)} %bitcast.4, bf16[1024,128]{1,0:T(8,128)(2,1)S(1)} %copy-done.1, f32[1,1024]{1,0:T(1,128)S(1)} %bitcast.5, f32[1,1024]{1,0:T(1,128)S(1)} %bitcast.6, s32[3,200,1024]{2,1,0:T(8,128)S(1)} %copy-done.3), custom_call_target="tpu_custom_call" | custom-call | flops 2000000000 | bytes 4000000 | tf_op jit(solution)/shard_map/sums/pallas_call | solution.py:234
  64.0 0.0 copy-start.6
  64.0 0.9 %copy-done.6 = f32[4,200,200]{2,1,0:T(8,128)} copy-done((f32[4,200,200]{2,1,0:T(8,128)}, f32[4,200,200]{2,1,0:T(8,128)S(1)}, u32[]{:S(2)}) %copy-start.6) | copy-done | bytes 640024
  64.9 14.8 %solve.1.change = f32[200,200]{1,0:T(8,128)} custom-call(f32[4,200,200]{2,1,0:T(8,128)} %copy-done.6), custom_call_target="tpu_custom_call" | custom-call | flops 20000000000 | bytes 60000000 | tf_op jit(solution)/shard_map/solve/pallas_call | solution.py:251
  79.7 0.0 collective-permute-done.2.refs_2_
  79.7 0.0 copy-start.7
  79.7 0.0 collective-permute-done.1.refs_1_
  79.7 0.0 copy-start.8
  79.7 0.0 collective-permute-done.refs_0_
  79.7 0.7 copy-done.7
  80.4 0.2 copy-done.8
  80.6 0.0 copy-start.9
  80.6 0.7 copy-done.9
  81.4 5.0 %final.1 = (bf16[200,512]{1,0:T(8,128)(2,1)}, f32[200,1024]{1,0:T(8,128)}) custom-call(f32[200,200]{1,0:T(8,128)} %solve.1.change, bf16[200,512]{1,0:T(8,128)(2,1)} %prior.3, s32[1,1024]{1,0:T(1,128)} %bitcast.3, bf16[1024,128]{1,0:T(8,128)(2,1)} %weights.3, f32[200,512]{1,0:T(8,128)} %copy-done.9, f32[200,512]{1,0:T(8,128)} %copy-done.8, f32[200,512]{1,0:T(8,128)} %copy-done.7), custom_call_target="tpu_custom_call" | custom-call | tf_op jit(solution)/shard_map/final/pallas_call | solution.py:260
Async XLA Ops:
  1.6 78.1 %collective-permute-start.2 = (f32[200,512]{1,0:T(8,128)S(1)}, f32[200,512]{1,0:T(8,128)S(1)}, u32[]{:S(2)}, u32[]{:S(2)}) collective-permute-start(f32[200,512]{1,0:T(8,128)S(1)} %convert_element_type.3), channel_id=1, source_target_pairs={{12,0},{0,4},{4,8},{8,12},{13,1},{1,5},{5,9},{9,13},{14,2},{2,6},{... | collective-permute-start | bytes 1228808 | tf_op jit(solution)/shard_map/ppermute | solution.py:227
  4.7 75.0 %collective-permute-start.1 = (f32[200,512]{1,0:T(8,128)S(1)}, f32[200,512]{1,0:T(8,128)S(1)}, u32[]{:S(2)}, u32[]{:S(2)}) collective-permute-start(f32[200,512]{1,0:T(8,128)S(1)} %convert_element_type.3), channel_id=1, source_target_pairs={{8,0},{12,4},{0,8},{4,12},{9,1},{13,5},{1,9},{5,13},{10,2},{14,6},... | collective-permute-start | bytes 1228808 | tf_op jit(solution)/shard_map/ppermute | solution.py:227
  7.3 72.4 %collective-permute-start = (f32[200,512]{1,0:T(8,128)S(1)}, f32[200,512]{1,0:T(8,128)S(1)}, u32[]{:S(2)}, u32[]{:S(2)}) collective-permute-start(f32[200,512]{1,0:T(8,128)S(1)} %convert_element_type.3), channel_id=1, source_target_pairs={{4,0},{8,4},{12,8},{0,12},{5,1},{9,5},{13,9},{1,13},{6,2},{10,6},{... | collective-permute-start | bytes 1228808 | tf_op jit(solution)/shard_map/ppermute | solution.py:227
  8.6 0.9 %copy-start = (bf16[200,512]{1,0:T(8,128)(2,1)S(1)}, bf16[200,512]{1,0:T(8,128)(2,1)}, u32[]{:S(2)}) copy-start(bf16[200,512]{1,0:T(8,128)(2,1)} %prior.3) | copy-start | bytes 614404
  9.6 0.9 %copy-start.1 = (bf16[1024,128]{1,0:T(8,128)(2,1)S(1)}, bf16[1024,128]{1,0:T(8,128)(2,1)}, u32[]{:S(2)}) copy-start(bf16[1024,128]{1,0:T(8,128)(2,1)} %weights.3) | copy-start | bytes 786436
  10.5 0.7 copy-start.2
  11.2 1.7 %copy-start.3 = (s32[3,200,1024]{2,1,0:T(8,128)S(1)}, s32[3,200,1024]{2,1,0:T(8,128)}, u32[]{:S(2)}) copy-start(s32[3,200,1024]{2,1,0:T(8,128)} %seeds.1) | copy-start | bytes 7372804
  12.9 0.7 copy-start.4
  13.6 0.7 copy-start.5
  64.0 0.9 %copy-start.6 = (f32[4,200,200]{2,1,0:T(8,128)}, f32[4,200,200]{2,1,0:T(8,128)S(1)}, u32[]{:S(2)}) copy-start(f32[4,200,200]{2,1,0:T(8,128)S(1)} %sums.1) | copy-start | bytes 1920004
  79.7 0.8 copy-start.7
  79.7 0.9 %copy-start.8 = (f32[200,512]{1,0:T(8,128)}, f32[200,512]{1,0:T(8,128)S(1)}, u32[]{:S(2)}) copy-start(f32[200,512]{1,0:T(8,128)S(1)} %collective-permute-done.1.refs_1_) | copy-start | bytes 1228804
  80.6 0.7 copy-start.9

commit v2 on v1

v2 whole, which is shorter than its diff:
```python
import functools

import jax
import jax.numpy as jnp
from jax import lax
from jax.experimental import pallas as pl
from jax.experimental.pallas import tpu as pltpu
from jax.sharding import PartitionSpec as P

BLK = 128
ITERS = 3
MESH = pl.DeviceIdType.MESH
VM = pl.BlockSpec(memory_space=pltpu.VMEM)
NN = (((1,), (0,)), ((), ()))
NT = (((1,), (1,)), ((), ()))


def mm(a, b, dims):
    return lax.dot_general(a, b, dims, preferred_element_type=jnp.float32)


def split(x):
    hi = x.astype(jnp.bfloat16)
    return hi, (x - hi.astype(jnp.float32)).astype(jnp.bfloat16)


def dot3(a, b, dims):
    ah, al = split(a)
    bh, bl = split(b)
    return mm(ah, bh, dims) + (mm(ah, bl, dims) + mm(al, bh, dims))


def dot_exact(a, b, dims):
    return lax.dot_general(a, b, dims, precision=lax.Precision.HIGHEST, preferred_element_type=jnp.float32)


def block_predictions(fields, weights, block):
    total = None
    for field, first in fields:
        for b in range(field.shape[1] // BLK):
            part = mm(field[:, b * BLK:(b + 1) * BLK].astype(jnp.bfloat16), weights[...], NT)
            here = block == first + b
            total = jnp.where(here, part, 0.0 if total is None else total)
    return total


def sums_kernel(n_cell, n_obs, sizes, prior_in, block_in, weights_in, observed_in, sigma_in, seeds_in, out, pred,
                prior, block, weights, observed, sigma, seeds, acc, fin, obs_recv, cell_recv, own, gath,
                load_sem, send_sem, recv_sem, gsend_sem, grecv_sem):
    loads = [
        pltpu.make_async_copy(a, b, load_sem.at[i])
        for i, (a, b) in enumerate(((prior_in, prior), (weights_in, weights), (block_in, block), (sigma_in, sigma),
                                    (observed_in, observed), (seeds_in, seeds)))
    ]
    for load in loads:
        load.start()
    members, width = prior.shape
    cell, obs = lax.axis_index("cell"), lax.axis_index("obs")
    bits = [1 << k for k in range(n_obs.bit_length() - 1)]
    barrier = pltpu.get_barrier_semaphore()
    for bit in bits:
        pl.semaphore_signal(barrier, inc=1, device_id={"obs": obs ^ bit}, device_id_type=MESH)
    for d in range(1, n_cell):
        pl.semaphore_signal(barrier, inc=1, device_id={"cell": lax.rem(cell + d, n_cell)}, device_id_type=MESH)

    nblocks = width // BLK
    first = cell * nblocks
    pieces, piece = gath.shape[0], gath.shape[3]
    part = obs & (pieces - 1)
    gbits = [pieces >> (k + 1) for k in range(pieces.bit_length() - 1)]
    held = [0]
    gflights = []

    def remote(src, dst, send, recv, to):
        return pltpu.make_async_remote_copy(src_ref=src, dst_ref=dst, send_sem=send, recv_sem=recv, device_id=to,
                                            device_id_type=MESH)

    def add_blocks(slots):
        blk = block[...]
        for slot in slots:
            for d in range(1, n_cell):
                source = lax.rem(cell + n_cell - d, n_cell) * nblocks + slot * (piece // BLK)
                for b in range(piece // BLK):
                    field = gath[slot, d - 1, :, b * BLK:(b + 1) * BLK].astype(jnp.bfloat16)
                    pred[...] = jnp.where(blk == source + b, mm(field, weights[...], NT), pred[...])

    def gather_start(g):
        if g == 0:
            for d in range(1, n_cell):
                gflights.append(remote(own, gath.at[part, d - 1], gsend_sem.at[g, d - 1], grecv_sem.at[g, d - 1],
                                       {"cell": lax.rem(cell + d, n_cell)}))
        else:
            for j, h in enumerate(held):
                gflights.append(remote(gath.at[part ^ h], gath.at[part ^ h], gsend_sem.at[g, j], grecv_sem.at[g, j],
                                       {"obs": obs ^ gbits[g - 1]}))
        for c in gflights:
            c.start()

    def gather_step(g):
        for c in gflights:
            c.wait()
        gflights.clear()
        fresh = [0] if g == 0 else [h ^ gbits[g - 1] for h in held]
        if g > 0:
            held.extend(fresh)
        if g < len(gbits):
            gather_start(g + 1)
        add_blocks([part ^ h for h in fresh])

    loads[0].wait()
    own[...] = prior[:, pl.ds(pl.multiple_of(part * piece, BLK), piece)].astype(jnp.float32)
    for load in loads[1:]:
        load.wait()
    blk = block[...]
    predicted = block_predictions([(prior, first)], weights, blk)
    pl.semaphore_wait(barrier, len(bits) + n_cell - 1)
    gather_start(0)
    pred[...] = predicted
    inside = jnp.logical_and(blk >= first, blk < first + nblocks)
    mean = jnp.mean(predicted, axis=0, keepdims=True)
    inv = 1.0 / sigma[...]
    dev = (predicted - mean) * jnp.where(inside, inv, 0.0)
    base = (observed[...] - mean) * inv + (3.0 / 1048576.0 - 3.0)
    ah, al = split(dev)
    scale = 1.0 / (members - 1.0)

    def put(k):
        if k == 0:
            h, l = ah, al
        else:
            h, l = split(base + seeds[k - 1].astype(jnp.float32) * (6.0 / 1048576.0))
        acc[k * members:(k + 1) * members, 0:members] = (mm(h, ah, NT) + (mm(h, al, NT) + mm(l, ah, NT))) * scale

    nbit = len(bits)
    bases = [sum(sizes[:s]) for s in range(len(sizes))]
    lens = [[size >> k for k in range(nbit + 1)] for size in sizes]
    offs = []
    for s, base_row in enumerate(bases):
        at = [jnp.int32(base_row)]
        for k in range(nbit):
            at.append(pl.multiple_of(at[-1] + ((obs >> k) & 1) * lens[s][k + 1], 8))
        offs.append(at)
    stages = 2 * nbit + 2

    def copies(s, stage):
        made = []
        chunk = lens[s][-1] // n_cell
        if stage < nbit:
            n = lens[s][stage + 1]
            src = pl.multiple_of(offs[s][stage] + (1 - ((obs >> stage) & 1)) * n, 8)
            made.append((acc.at[pl.ds(src, n)], obs_recv.at[pl.ds(bases[s] + sizes[s] - 2 * n, n)], {"obs": obs ^ bits[stage]}))
        elif stage == nbit:
            for d in range(1, n_cell):
                to = lax.rem(cell + d, n_cell)
                src = pl.multiple_of(offs[s][-1] + to * chunk, 8)
                made.append((acc.at[pl.ds(src, chunk)], cell_recv.at[s, d - 1, pl.ds(0, chunk)], {"cell": to}))
        elif stage == nbit + 1:
            mine = pl.ds(pl.multiple_of(offs[s][-1] + cell * chunk, 8), chunk)
            for d in range(1, n_cell):
                made.append((fin.at[mine], fin.at[mine], {"cell": lax.rem(cell + d, n_cell)}))
        else:
            k = stages - 1 - stage
            mine = pl.ds(offs[s][k + 1], lens[s][k + 1])
            made.append((fin.at[mine], fin.at[mine], {"obs": obs ^ bits[k]}))
        return [remote(a, b, send_sem.at[s, stage, j], recv_sem.at[s, stage, j], to) for j, (a, b, to) in enumerate(made)]

    flights = {}

    def start(s, stage):
        flights[s, stage] = copies(s, stage)
        for c in flights[s, stage]:
            c.start()

    def finish(s, stage):
        for c in flights[s, stage]:
            c.wait()
        if stage < nbit:
            n = lens[s][stage + 1]
            mine = pl.ds(offs[s][stage + 1], n)
            acc[mine] = acc[mine] + obs_recv[pl.ds(bases[s] + sizes[s] - 2 * n, n)]
        elif stage == nbit:
            chunk = lens[s][-1] // n_cell
            mine = pl.ds(pl.multiple_of(offs[s][-1] + cell * chunk, 8), chunk)
            total = acc[mine]
            for d in range(1, n_cell):
                total = total + cell_recv[s, d - 1, pl.ds(0, chunk)]
            fin[mine] = total

    acc[...] = jnp.zeros_like(acc)
    done = 0
    for s in range(len(sizes)):
        while done < ITERS + 1 and done * members < bases[s] + sizes[s]:
            put(done)
            done += 1
        if s == 0:
            start(0, 0)
    second = len(sizes) > 1
    gathers = 0
    for stage in range(stages + 1):
        if stage < stages:
            finish(0, stage)
            if stage + 1 < stages:
                start(0, stage + 1)
        if second:
            if stage > 0:
                finish(1, stage - 1)
            if stage < stages:
                start(1, stage)
        if stage % 2 == 1 and gathers <= len(gbits):
            gather_step(gathers)
            gathers += 1
    while gathers <= len(gbits):
        gather_step(gathers)
        gathers += 1
    for k in range(ITERS + 1):
        out[k] = fin[k * members:(k + 1) * members, 0:members]


def solve_kernel(sums_in, prior_in, predicted_in, posterior, post_predicted, sums, prior, predicted, result, stack,
                 dev_op, load_sem):
    loads = [
        pltpu.make_async_copy(a, b, load_sem.at[i])
        for i, (a, b) in enumerate(((sums_in, sums), (prior_in, prior), (predicted_in, predicted)))
    ]
    for load in loads:
        load.start()
    loads[0].wait()
    members = result.shape[0]
    row = lax.broadcasted_iota(jnp.int32, (members, members), 0)
    col = lax.broadcasted_iota(jnp.int32, (members, members), 1)
    eye = jnp.where(row == col, 1.0, 0.0)
    inflation = float(ITERS)
    up, down = pl.ds(0, members), pl.ds(members, members)

    def solve(gram, cross):
        system = gram + inflation * eye
        bound = jnp.max(jnp.sum(jnp.abs(system), axis=1))
        scale = 2.0 / (inflation + bound)
        stack[up] = eye - scale * system
        stack[down] = scale * cross

        def loop(dot):
            def body(carry):
                step, _ = carry
                residue = stack[up]
                size = jnp.sum(residue * residue)
                moved = dot(stack[...], residue, NN)
                stack[down] = stack[down] + moved[members:]
                stack[up] = moved[:members]
                return step + 1, size

            lax.while_loop(lambda c: jnp.logical_and(c[0] < 64, c[1] > 1e-6), body, (jnp.int32(0), jnp.float32(1e9)))

        pl.when(bound <= 300.0)(lambda: loop(dot3))
        pl.when(jnp.logical_not(bound <= 300.0))(lambda: loop(dot_exact))
        return stack[down]

    gram0 = sums[0]
    change = solve(gram0, sums[1] - gram0)
    change = change - jnp.mean(change, axis=1, keepdims=True)
    result[...] = change
    for i in range(1, ITERS):
        change = result[...]
        dev_op[...] = eye + change - jnp.mean(eye + change, axis=0, keepdims=True)
        stack[up] = sums[0] + dot3(change, sums[0], NN)
        stack[down] = sums[1 + i]
        both = dot3(stack[...], dev_op[...], NT)
        v = both[:members]
        z = solve(v - jnp.mean(v, axis=0, keepdims=True), both[members:] - v)
        result[...] = result[...] + dot3(z, dev_op[...], NN)
    shift = result[...]
    for load in loads[1:]:
        load.wait()
    field = prior[...].astype(jnp.float32)
    field_dev = field - jnp.mean(field, axis=0, keepdims=True)
    posterior[...] = (field + dot3(shift, field_dev, NN)).astype(jnp.bfloat16)
    first = predicted[...]
    post_predicted[...] = first + dot3(shift, first - jnp.mean(first, axis=0, keepdims=True), NN)


def per_device(n_cell, n_obs, prior, obs_block, obs_weight, observed, obs_sigma, pert_seed):
    members, width = prior.shape
    count = obs_block.shape[0]
    block, observed, sigma = (x.reshape(1, count) for x in (obs_block, observed, obs_sigma))
    unit = 8 * n_cell * n_obs
    units = -(-(ITERS + 1) * members // unit)
    sizes = [unit * (units - units // 2), unit * (units // 2)] if units > 1 else [unit]
    rows = sum(sizes)
    lanes = -(-members // 128) * 128
    stages = 2 * (n_obs.bit_length() - 1) + 2
    pieces = min(n_obs, width // BLK)
    piece = width // pieces
    f32 = jnp.float32
    hbm = pl.BlockSpec(memory_space=pltpu.HBM)
    gstages = pieces.bit_length()
    gcopies = max(n_cell - 1, pieces)
    sums, predicted = pl.pallas_call(
        functools.partial(sums_kernel, n_cell, n_obs, sizes),
        out_shape=(jax.ShapeDtypeStruct((ITERS + 1, members, members), f32),
                   jax.ShapeDtypeStruct((members, count), f32)),
        in_specs=[hbm] * 6,
        out_specs=(VM, VM),
        scratch_shapes=[
            pltpu.VMEM(prior.shape, prior.dtype),
            pltpu.VMEM(block.shape, block.dtype),
            pltpu.VMEM(obs_weight.shape, obs_weight.dtype),
            pltpu.VMEM(observed.shape, f32),
            pltpu.VMEM(sigma.shape, f32),
            pltpu.VMEM(pert_seed.shape, pert_seed.dtype),
            pltpu.VMEM((rows, lanes), f32),
            pltpu.VMEM((rows, lanes), f32),
            pltpu.VMEM((rows, lanes), f32),
            pltpu.VMEM((len(sizes), n_cell - 1, sizes[0] // n_obs // n_cell, lanes), f32),
            pltpu.VMEM((members, piece), f32),
            pltpu.VMEM((pieces, n_cell - 1, members, piece), f32),
            pltpu.SemaphoreType.DMA((6,)),
            pltpu.SemaphoreType.DMA((len(sizes), stages, n_cell - 1)),
            pltpu.SemaphoreType.DMA((len(sizes), stages, n_cell - 1)),
            pltpu.SemaphoreType.DMA((gstages, gcopies)),
            pltpu.SemaphoreType.DMA((gstages, gcopies)),
        ],
        compiler_params=pltpu.CompilerParams(collective_id=0, has_side_effects=True, vmem_limit_bytes=67043328),
        name="sums",
    )(prior, block, obs_weight, observed, sigma, pert_seed)
    return pl.pallas_call(
        solve_kernel,
        out_shape=(jax.ShapeDtypeStruct((members, width), jnp.bfloat16),
                   jax.ShapeDtypeStruct((members, count), f32)),
        in_specs=[hbm] * 3,
        out_specs=(VM, VM),
        scratch_shapes=[
            pltpu.VMEM(sums.shape, f32),
            pltpu.VMEM(prior.shape, prior.dtype),
            pltpu.VMEM(predicted.shape, f32),
            pltpu.VMEM((members, members), f32),
            pltpu.VMEM((2 * members, members), f32),
            pltpu.VMEM((members, members), f32),
            pltpu.SemaphoreType.DMA((3,)),
        ],
        compiler_params=pltpu.CompilerParams(vmem_limit_bytes=67043328),
        name="solve",
    )(sums, prior, predicted)


def solution(mesh):
    return jax.shard_map(
        functools.partial(per_device, mesh.shape["cell"], mesh.shape["obs"]),
        mesh=mesh,
        in_specs=(
            P("scen", "cell"),
            P("obs"),
            P("obs", None),
            P(("scen", "obs")),
            P("obs"),
            P("scen", None, "obs"),
        ),
        out_specs=(P("scen", "cell"), P("scen", "obs")),
        check_vma=False,
    )
```

time: 86.5 us -> 53.4 us (0.62)
  Pallas kernels: 69.5 us -> 53.3 us
  local copies, waits for them, and re-layouts: 8.16 us -> 0 us
  starting transfers between devices: 7.04 us -> 0 us
  other arithmetic: 0.97 us -> 0 us
    pallas_call x3 -> x2, Pallas kernels: 69.5 us -> 53.3 us  [the longest x1 37 us: per_device(): pl.pallas_call(functools.partial(sums_kernel, n_cell, n_obs, sizes), out_...]
    unnamed x20 -> x0, local copies, waits for them, and re-layouts: 8.16 us -> none
    ppermute x3 -> x0, starting transfers between devices: 7.04 us -> none  [per_device(): lax.ppermute(wide, 'cell', [((i + d) % n_cell, i) for i in range(n_cell)])]
    convert_element_type x1 -> x0, other arithmetic: 0.97 us -> none  [per_device(): wide = prior.astype(jnp.float32)]
  transfers between devices with their start and end apart: 3 -> 0, of which waited for: 0 -> 0; matrix products, arithmetic and copies ran while one was open for 0% -> 0% of each run, Pallas kernels for 75% -> 0%
where the time goes in v2:
time: 53.4 us; the launch traced here: 53.9 us
  Pallas kernels  53.3 us (100%)
  between operations  0.64 us (1%)
    pallas_call x1, Pallas kernels, per_device(): pl.pallas_call(functools.partial(sums_kernel, n_cell, n_obs, sizes), out_...  37 us
    pallas_call x1, Pallas kernels, per_device(): pl.pallas_call(solve_kernel, out_shape=(jax.ShapeDtypeStruct((members, wi...  16.3 us

profile of v2, /device:TPU:0, one launch (start us, length us, event | category | flops | bytes accessed | tf_op | source)
XLA Modules:
  0.0 53.9 jit_solution(5849725664107407770)
XLA Ops:
  0.6 37.0 %sums.1 = (f32[4,200,200]{2,1,0:T(8,128)}, f32[200,1024]{1,0:T(8,128)}) custom-call(bf16[200,512]{1,0:T(8,128)(2,1)} %prior_in.3, s32[1,1024]{1,0:T(1,128)} %bitcast.3, bf16[1024,128]{1,0:T(8,128)(2,1)} %weights_in.1, f32[1,1024]{1,0:T(1,128)} %bitcast.4, f32[1,1024]{1,0:T(1,128)} %bitcast.5, s32[3,200,1024]{2,1,0:T(8,128)} %seeds_in.1), custom_call_target="tpu_custom_call" | custom-call | tf_op jit(solution)/shard_map/sums/pallas_call | solution.py:297
  37.6 16.3 %solve.1 = (bf16[200,512]{1,0:T(8,128)(2,1)}, f32[200,1024]{1,0:T(8,128)}) custom-call(f32[4,200,200]{2,1,0:T(8,128)} %get-tuple-element.4.sums_in, bf16[200,512]{1,0:T(8,128)(2,1)} %prior_in.3, f32[200,1024]{1,0:T(8,128)} %get-tuple-element.5.predicted_in), custom_call_target="tpu_custom_call" | custom-call | tf_op jit(solution)/shard_map/solve/pallas_call | solution.py:325

commit v3 on v2

--- a/solution.py
+++ b/solution.py
@@ -109,7 +109,7 @@
 
     loads[0].wait()
     own[...] = prior[:, pl.ds(pl.multiple_of(part * piece, BLK), piece)].astype(jnp.float32)
-    for load in loads[1:]:
+    for load in loads[1:5]:
         load.wait()
     blk = block[...]
     predicted = block_predictions([(prior, first)], weights, blk)
@@ -187,26 +187,23 @@
             fin[mine] = total
 
     acc[...] = jnp.zeros_like(acc)
-    done = 0
-    for s in range(len(sizes)):
+    put(0)
+    loads[5].wait()
+    done, count = 1, len(sizes)
+    for s in range(count):
         while done < ITERS + 1 and done * members < bases[s] + sizes[s]:
             put(done)
             done += 1
-        if s == 0:
-            start(0, 0)
-    second = len(sizes) > 1
+        start(s, 0)
     gathers = 0
-    for stage in range(stages + 1):
-        if stage < stages:
-            finish(0, stage)
-            if stage + 1 < stages:
-                start(0, stage + 1)
-        if second:
-            if stage > 0:
-                finish(1, stage - 1)
-            if stage < stages:
-                start(1, stage)
-        if stage % 2 == 1 and gathers <= len(gbits):
+    for step in range(stages + count - 1):
+        for s in range(count):
+            stage = step - s
+            if 0 <= stage < stages:
+                finish(s, stage)
+                if stage + 1 < stages:
+                    start(s, stage + 1)
+        if step >= count - 1 and (step - count) % 3 == 2 and gathers <= len(gbits):
             gather_step(gathers)
             gathers += 1
     while gathers <= len(gbits):
@@ -284,7 +281,8 @@
     block, observed, sigma = (x.reshape(1, count) for x in (obs_block, observed, obs_sigma))
     unit = 8 * n_cell * n_obs
     units = -(-(ITERS + 1) * members // unit)
-    sizes = [unit * (units - units // 2), unit * (units // 2)] if units > 1 else [unit]
+    count_sets = min(3, units)
+    sizes = [unit * (units // count_sets + (s < units % count_sets)) for s in range(count_sets)]
     rows = sum(sizes)
     lanes = -(-members // 128) * 128
     stages = 2 * (n_obs.bit_length() - 1) + 2

time: 53.4 us -> 56.4 us (1.056); the launches traced: 53.9 us -> 55.9 us
  Pallas kernels: 53.3 us -> 55.3 us
    pallas_call x1, Pallas kernels: 37 us -> 39.8 us  [per_device(): pl.pallas_call(functools.partial(sums_kernel, n_cell, n_obs, sizes), out_...]
    pallas_call x1, Pallas kernels: 16.3 us -> 15.5 us  [per_device(): pl.pallas_call(solve_kernel, out_shape=(jax.ShapeDtypeStruct((members, wi...]
where the time goes in v3:
time: 56.4 us; the launch traced here: 55.9 us
  Pallas kernels  55.3 us (98%)
  between operations  0.64 us (1%)
    pallas_call x1, Pallas kernels, per_device(): pl.pallas_call(functools.partial(sums_kernel, n_cell, n_obs, sizes), out_...  39.8 us
    pallas_call x1, Pallas kernels, per_device(): pl.pallas_call(solve_kernel, out_shape=(jax.ShapeDtypeStruct((members, wi...  15.5 us

profile of v3, /device:TPU:0, one launch (start us, length us, event | category | flops | bytes accessed | tf_op | source)
XLA Modules:
  0.0 55.9 jit_solution(2412368590892906159)
XLA Ops:
  0.6 39.8 %sums.1 = (f32[4,200,200]{2,1,0:T(8,128)}, f32[200,1024]{1,0:T(8,128)}) custom-call(bf16[200,512]{1,0:T(8,128)(2,1)} %prior_in.3, s32[1,1024]{1,0:T(1,128)} %bitcast.3, bf16[1024,128]{1,0:T(8,128)(2,1)} %weights_in.1, f32[1,1024]{1,0:T(1,128)} %bitcast.4, f32[1,1024]{1,0:T(1,128)} %bitcast.5, s32[3,200,1024]{2,1,0:T(8,128)} %seeds_in.1), custom_call_target="tpu_custom_call" | custom-call | tf_op jit(solution)/shard_map/sums/pallas_call | solution.py:295
  40.4 15.5 %solve.1 = (bf16[200,512]{1,0:T(8,128)(2,1)}, f32[200,1024]{1,0:T(8,128)}) custom-call(f32[4,200,200]{2,1,0:T(8,128)} %get-tuple-element.4.sums_in, bf16[200,512]{1,0:T(8,128)(2,1)} %prior_in.3, f32[200,1024]{1,0:T(8,128)} %get-tuple-element.5.predicted_in), custom_call_target="tpu_custom_call" | custom-call | tf_op jit(solution)/shard_map/solve/pallas_call | solution.py:323
